TPU v7x, 32 devices: a whole 2x2x4 slice. The times are simulated.
32 devices in a mesh: blk: 8 (over z, x), ga: 4 (over y, core).
Axes of the slice: x: 2, y: 2, z: 4, core: 2. Of those that a mesh axis runs over, the one named last changes fastest.
Arguments:
- pair_val: bfloat16 [16, 16, 16, 2048], P('blk', None, None, 'ga'), may hold values from -0.125 to 0.125
- pair_con: bfloat16 [16, 16, 16, 2048], P('blk', None, None, 'ga'), may hold values from -6 to 6
- screened: bfloat16 [16, 2048, 2048], P('blk', None, 'ga'), may hold values from -0.125 to 0.125
- amplitude: bfloat16 [16, 16], P('blk'), may hold values from -6 to 6
- qmap: int32 [16, 16], P('blk'), may hold values from 0 to 15, as said below
Outputs:
- kernel_x: float32 [16, 16], P('blk')
Inputs may be any that keep to these rules, and one draw needn't show every extreme that they name: qmap[k, k'] is the label of the difference k - k' (periodic) on a grid of 8 by 2 points, with the points and the differences labelled at random; every row and every column holds each label once.
All inputs are finite; a program needn't handle non-finite values.
Results may differ from a plain program's by a relative error of at most 0.004.
Values may be sent and summed in bfloat16 or wider, within the bound.
No kernel may reach another device: no remote copies, remote signals or barrier semaphores. Data moves between devices by JAX's collectives and lax.ppermute only.
A program may use at most 64 MiB of HBM per device.

v0:
```python
import jax
import jax.numpy as jnp
from jax import lax
from jax.sharding import PartitionSpec as P

NV = 4
NC = 4


def inverse_rows(qmap):
    total = qmap.shape[1]
    labels = jnp.arange(total, dtype=jnp.int32)
    hits = (qmap[:, :, None] == labels[None, None, :]).astype(jnp.int32)
    return jnp.sum(hits * labels[None, :, None], axis=1)


def swap(value, axis, size, step):
    return lax.ppermute(value, axis, [(i, i ^ step) for i in range(size)])


def body_of(blk, ga):

    def body(pair_val, pair_con, screened, amplitude, qmap):
        local_k, total, band_pairs, width = pair_val.shape
        local_q = screened.shape[0]
        slot = lax.axis_index("ga")
        every_amp = lax.all_gather(amplitude, "blk", axis=0, tiled=True)
        partner = inverse_rows(qmap)
        con_sorted = jnp.take_along_axis(pair_con, partner[:, :, None, None], axis=1)
        con_sorted, every_amp = lax.optimization_barrier((con_sorted, every_amp))
        con_in = lax.all_to_all(con_sorted, "blk", split_axis=1, concat_axis=0, tiled=True)
        val_sorted = jnp.take_along_axis(pair_val, partner[:, :, None, None], axis=1)
        amp_sorted = every_amp[partner].reshape(local_k, total, NV, NC)
        val_five = val_sorted.reshape(local_k, total, NV, NV, width)
        zeta = jnp.einsum(
            "kqavg,kqvc->kqacg", val_five, amp_sorted, preferred_element_type=jnp.float32
        )
        zeta = zeta.astype(jnp.bfloat16).reshape(local_k, total, NV * NC, width)
        far = swap(con_in, "ga", ga, ga // 2)
        near = swap(con_in, "ga", ga, 1)
        zeta_in = lax.all_to_all(zeta, "blk", split_axis=1, concat_axis=0, tiled=True)
        pieces = {0: con_in, 1: near, ga // 2: far, ga // 2 + 1: swap(far, "ga", ga, 1)}
        weights = screened.reshape(local_q, ga, width, screened.shape[2])
        unit = 0.0
        for key, held in pieces.items():
            block = lax.dynamic_index_in_dim(weights, slot ^ key, 1, keepdims=False)
            unit = unit + jnp.einsum(
                "kqxg,qgh->kqxh", held, block, preferred_element_type=jnp.float32
            )
        unit = unit.astype(jnp.bfloat16).reshape(total, local_q, NC, NC, -1)
        zeta = zeta_in.reshape(total, local_q, NV, NC, -1)
        terms = jnp.einsum("kqcyg,kqayg->kac", unit, zeta, preferred_element_type=jnp.float32)
        terms = terms.reshape(blk, 1, local_k, NV * NC)
        terms = jnp.broadcast_to(terms, (blk, ga, local_k, NV * NC)).reshape(
            blk * ga, local_k, NV * NC
        )
        back = lax.all_to_all(terms, ("blk", "ga"), split_axis=0, concat_axis=0, tiled=True)
        return jnp.sum(back, 0) / total

    return body


def solution(mesh):
    placed = (
        P("blk", None, None, "ga"),
        P("blk", None, None, "ga"),
        P("blk", None, "ga"),
        P("blk", None),
        P("blk", None),
    )
    return jax.shard_map(
        body_of(mesh.shape["blk"], mesh.shape["ga"]),
        mesh=mesh,
        in_specs=placed,
        out_specs=P("blk", None),
        check_vma=False,
    )
```

profile of v0, /device:TPU:0, one launch (start us, length us, event | category | flops | bytes accessed | tf_op | source)
XLA Modules:
  0.0 74.7 jit_solution(2706167675406388047)
XLA Ops:
  0.0 0.8 %select_reduce_fusion = s32[2,16]{1,0:T(2,128)S(1)} fusion(s32[2,16]{1,0:T(2,128)} %param.11), kind=kLoop, calls=%fused_computation.24 | loop fusion | flops 1504 | bytes 256 | tf_op jit(solution)/shard_map/reduce_sum | solution.py:14
  1.1 0.6 gather_fusion.2
  1.7 1.7 %gather_fusion.1 = bf16[32,16,512]{2,1,0:T(8,128)(2,1)S(1)} fusion(bf16[2,16,16,512]{3,2,1,0:T(8,128)(2,1)} %param.8, s32[32]{0:T(128)S(1)} %reshape.99), kind=kCustom, calls=%fused_computation.clone | custom fusion | bytes 1048832 | tf_op jit(solution)/shard_map/jit(take_along_axis)/gather | solution.py:29
  3.4 22.4 %all-gather = bf16[8,2,16]{2,1,0:T(2,128)(2,1)S(1)} all-gather(bf16[1,2,16]{2,1,0:T(2,128)(2,1)} %bitcast.98), channel_id=1, replica_groups=mesh['blk'=8,'ga'=4] {'blk'}, dimensions={0}, use_global_device_ids=true | all-gather | bytes 576 | tf_op jit(solution)/shard_map/all_gather | solution.py:27
  25.8 0.2 broadcast_select_fusion
  26.0 0.8 %copy.96 = bf16[2,16,16,512]{3,2,0,1:T(8,128)(2,1)} copy(bf16[2,16,16,512]{3,2,1,0:T(8,128)(2,1)S(1)} %get-tuple-element.9) | data formatting | bytes 1048576 | tf_op jit(solution)/shard_map/optimization_barrier | solution.py:30
  26.8 3.5 %all-to-all-start.1 = ((bf16[2,16,16,512]{3,2,0,1:T(8,128)(2,1)}), bf16[2,16,16,512]{3,2,0,1:T(8,128)(2,1)S(1)}, u32[]{:S(2)}, u32[]{:S(2)}) async-start(bf16[2,16,16,512]{3,2,0,1:T(8,128)(2,1)} %copy.96), calls=%async_computation.1 | async-start | bytes 1048576 | tf_op jit(solution)/shard_map/all_to_all | solution.py:31
  30.4 0.6 gather_fusion
  31.4 0.4 fusion.2
  32.0 0.8 %copy.92 = bf16[2,16,16,512]{3,2,0,1:T(8,128)(2,1)} copy(bf16[2,16,16,512]{3,2,1,0:T(8,128)(2,1)S(1)} %reshape.58) | data formatting | bytes 1048576 | tf_op jit(solution)/shard_map/reshape | solution.py:38
  32.8 8.4 %all-to-all-done.1 = bf16[2,16,16,512]{3,2,0,1:T(8,128)(2,1)S(1)} async-done(((bf16[2,16,16,512]{3,2,0,1:T(8,128)(2,1)}), bf16[2,16,16,512]{3,2,0,1:T(8,128)(2,1)S(1)}, u32[]{:S(2)}, u32[]{:S(2)}) %all-to-all-start.1) | async-done | bytes 524320 | tf_op jit(solution)/shard_map/all_to_all | solution.py:31
  41.2 3.7 %all-to-all-start = ((bf16[2,16,16,512]{3,2,0,1:T(8,128)(2,1)}), bf16[2,16,16,512]{3,2,0,1:T(8,128)(2,1)S(1)}, u32[]{:S(2)}, u32[]{:S(2)}) async-start(bf16[2,16,16,512]{3,2,0,1:T(8,128)(2,1)} %copy.92), calls=%async_computation | async-start | bytes 1048576 | tf_op jit(solution)/shard_map/all_to_all | solution.py:41
  45.0 1.6 %collective-permute-start.1 = (bf16[16,2,16,512]{3,2,0,1:T(8,128)(2,1)S(1)}, bf16[16,2,16,512]{3,2,0,1:T(8,128)(2,1)S(1)}, u32[]{:S(2)}, u32[]{:S(2)}) collective-permute-start(bf16[16,2,16,512]{3,2,0,1:T(8,128)(2,1)S(1)} %bitcast.92), channel_id=1, source_target_pairs={{0,2},{1,3},{2,0},{3,1},{4,6},{5,7},{6,4},{7,5},{8,10},{9,11},{10,... | collective-permute-start | bytes 1572872 | tf_op jit(solution)/shard_map/ppermute | solution.py:18
  46.5 10.8 %all-to-all-done = bf16[2,16,16,512]{3,2,0,1:T(8,128)(2,1)S(1)} async-done(((bf16[2,16,16,512]{3,2,0,1:T(8,128)(2,1)}), bf16[2,16,16,512]{3,2,0,1:T(8,128)(2,1)S(1)}, u32[]{:S(2)}, u32[]{:S(2)}) %all-to-all-start) | async-done | bytes 524320 | tf_op jit(solution)/shard_map/all_to_all | solution.py:41
  57.3 0.5 copy.94
  57.9 1.8 %fusion.6 = f32[2,512,16,16]{1,3,2,0:T(8,128)S(1)} fusion(bf16[16,2,16,512]{3,2,0,1:T(8,128)(2,1)S(1)} %bitcast.94, bf16[2,4,512,512]{3,2,1,0:T(8,128)(2,1)} %bitcast.99, s32[]{:T(128)S(6)} %select_n.30), kind=kOutput, calls=%fused_computation.14 | convolution fusion | flops 268435456 | bytes 2621444 | tf_op jit(solution)/shard_map/kqxg,qgh->kqxh/dot_general | solution.py:47
  59.8 0.6 copy-done.1
  60.4 0.4 convolution_add_fusion.2
  60.9 0.5 convolution_add_fusion.1
  61.3 0.4 collective-permute-done.2
  61.7 0.4 fusion.1
  62.3 0.9 %convolution_bitcast_fusion = f32[16,4,4]{2,1,0:T(4,128)S(1)} fusion(bf16[16,2,4,4,512]{4,3,2,0,1:T(4,128)(2,1)S(1)} %reshape.61, bf16[16,2,4,4,512]{4,1,3,2,0:T(2,128)(2,1)S(1)} %bitcast.95), kind=kOutput, calls=%fused_computation.10 | convolution fusion | flops 2097152 | bytes 1049600 | tf_op jit(solution)/shard_map/kqcyg,kqayg->kac/dot_general | solution.py:52
  63.3 10.8 %all_to_all.38 = f32[32,2,16]{2,1,0:T(2,128)S(1)} all-to-all(f32[32,2,16]{2,1,0:T(2,128)S(1)} %copy.105), channel_id=1, replica_groups=mesh['blk'=8,'ga'=4] {'blk','ga'}, dimensions={0} | all-to-all | bytes 8192 | tf_op jit(solution)/shard_map/all_to_all | solution.py:57
  74.2 0.6 broadcast_multiply_fusion
  (24 shorter events, 1.3 us)
Async XLA Ops:
  0.0 1.1 %copy-start = (bf16[2,16,16,512]{3,2,1,0:T(8,128)(2,1)S(1)}, bf16[2,16,16,512]{3,2,1,0:T(8,128)(2,1)}, u32[]{:S(2)}) copy-start(bf16[2,16,16,512]{3,2,1,0:T(8,128)(2,1)} %param.7) | copy-start | bytes 1572868
  26.8 14.4 %all-to-all-start.1 = ((bf16[2,16,16,512]{3,2,0,1:T(8,128)(2,1)}), bf16[2,16,16,512]{3,2,0,1:T(8,128)(2,1)S(1)}, u32[]{:S(2)}, u32[]{:S(2)}) async-start(bf16[2,16,16,512]{3,2,0,1:T(8,128)(2,1)} %copy.96), calls=%async_computation.1 | async-start | bytes 1048576 | tf_op jit(solution)/shard_map/all_to_all | solution.py:31
  41.2 16.1 %all-to-all-start = ((bf16[2,16,16,512]{3,2,0,1:T(8,128)(2,1)}), bf16[2,16,16,512]{3,2,0,1:T(8,128)(2,1)S(1)}, u32[]{:S(2)}, u32[]{:S(2)}) async-start(bf16[2,16,16,512]{3,2,0,1:T(8,128)(2,1)} %copy.92), calls=%async_computation | async-start | bytes 1048576 | tf_op jit(solution)/shard_map/all_to_all | solution.py:41
  45.0 14.8 %collective-permute-start.1 = (bf16[16,2,16,512]{3,2,0,1:T(8,128)(2,1)S(1)}, bf16[16,2,16,512]{3,2,0,1:T(8,128)(2,1)S(1)}, u32[]{:S(2)}, u32[]{:S(2)}) collective-permute-start(bf16[16,2,16,512]{3,2,0,1:T(8,128)(2,1)S(1)} %bitcast.92), channel_id=1, source_target_pairs={{0,2},{1,3},{2,0},{3,1},{4,6},{5,7},{6,4},{7,5},{8,10},{9,11},{10,... | collective-permute-start | bytes 1572872 | tf_op jit(solution)/shard_map/ppermute | solution.py:18
  46.5 13.3 %collective-permute-start = (bf16[16,2,16,512]{3,2,0,1:T(8,128)(2,1)S(1)}, bf16[16,2,16,512]{3,2,0,1:T(8,128)(2,1)S(1)}, u32[]{:S(2)}, u32[]{:S(2)}) collective-permute-start(bf16[16,2,16,512]{3,2,0,1:T(8,128)(2,1)S(1)} %bitcast.93), channel_id=1, source_target_pairs={{0,1},{1,0},{2,3},{3,2},{4,5},{5,4},{6,7},{7,6},{8,9},{9,8},{10,11... | collective-permute-start | bytes 1572872 | tf_op jit(solution)/shard_map/ppermute | solution.py:18
  57.9 2.5 %copy-start.1 = (bf16[2,2048,512]{2,1,0:T(8,128)(2,1)S(1)}, bf16[2,2048,512]{2,1,0:T(8,128)(2,1)}, u32[]{:S(2)}) copy-start(bf16[2,2048,512]{2,1,0:T(8,128)(2,1)} %param.9) | copy-start | bytes 12582916
  59.7 2.0 %collective-permute-start.2 = (bf16[16,2,16,512]{3,2,0,1:T(8,128)(2,1)S(1)}, bf16[16,2,16,512]{3,2,0,1:T(8,128)(2,1)S(1)}, u32[]{:S(2)}, u32[]{:S(2)}) collective-permute-start(bf16[16,2,16,512]{3,2,0,1:T(8,128)(2,1)S(1)} %collective-permute-done.1), channel_id=1, source_target_pairs={{0,1},{1,0},{2,3},{3,2},{4,5},{5,4},{6,7},{7,6},{8,9},{9,8},{10,11... | collective-permute-start | bytes 1572872 | tf_op jit(solution)/shard_map/ppermute | solution.py:18
where the time goes:
time: 75.1 us; the launch traced here: 74.7 us
  blocking collectives  33.2 us (44%)
  waiting for transfers between devices  19.6 us (26%)
  starting transfers between devices  8.84 us (12%)
  local copies, waits for them, and re-layouts  6.81 us (9%)
  matrix products  4.45 us (6%)
  other arithmetic  1.62 us (2%)
    all_gather x1, blocking collectives, body(): every_amp = lax.all_gather(amplitude, 'blk', axis=0, tiled=True)  22.4 us
    all_to_all x1, waiting for transfers between devices, body(): lax.all_to_all(zeta, 'blk', split_axis=1, concat_axis=0, tiled=True)  10.8 us
    all_to_all x1, blocking collectives, body(): lax.all_to_all(terms, ('blk', 'ga'), split_axis=0, concat_axis=0, tiled=T...  10.8 us
    all_to_all x1, waiting for transfers between devices, body(): lax.all_to_all(con_sorted, 'blk', split_axis=1, concat_axis=0, tiled=True)  8.4 us
    all_to_all x1, starting transfers between devices, body(): lax.all_to_all(zeta, 'blk', split_axis=1, concat_axis=0, tiled=True)  3.69 us
    all_to_all x1, starting transfers between devices, body(): lax.all_to_all(con_sorted, 'blk', split_axis=1, concat_axis=0, tiled=True)  3.49 us
    dot_general x4, matrix products, body(): jnp.einsum('kqxg,qgh->kqxh', held, block, preferred_element_type=jnp.floa...  3.15 us
    gather x2, local copies, waits for them, and re-layouts, body(): jnp.take_along_axis(pair_con, partner[:, :, None, None], axis=1)  1.75 us
  transfers between devices with their start and end apart: 5, of which 3 were waited for; matrix products, arithmetic and copies ran while one was open for 8% of the time, Pallas kernels for 0%

commit v1 on v0

--- a/solution.py
+++ b/solution.py
@@ -38,7 +38,10 @@
         zeta = zeta.astype(jnp.bfloat16).reshape(local_k, total, NV * NC, width)
         far = swap(con_in, "ga", ga, ga // 2)
         near = swap(con_in, "ga", ga, 1)
-        zeta_in = lax.all_to_all(zeta, "blk", split_axis=1, concat_axis=0, tiled=True)
+        zeta_in = jnp.concatenate(
+            lax.all_to_all(jnp.stack(jnp.split(zeta, lax.axis_size("blk"), axis=1)), "blk", 0, 0),
+            axis=0,
+        )
         pieces = {0: con_in, 1: near, ga // 2: far, ga // 2 + 1: swap(far, "ga", ga, 1)}
         weights = screened.reshape(local_q, ga, width, screened.shape[2])
         unit = 0.0

time: 75.1 us -> 73.9 us (0.984)
  waiting for transfers between devices: 19.6 us -> 15.8 us
  local copies, waits for them, and re-layouts: 6.81 us -> 10.5 us
  blocking collectives: 33.2 us -> 32.2 us
    ppermute x3, waiting for transfers between devices: 0.4 us -> 7.51 us  [swap(): return lax.ppermute(value, axis, [(i, i ^ step) for i in range(size)])]
    all_to_all x1, waiting for transfers between devices: 10.8 us -> 3.98 us  [body(): lax.all_to_all(jnp.stack(jnp.split(zeta, lax.axis_size('blk'), axis=1)),...]
    unnamed x4 -> x11, local copies, waits for them, and re-layouts: 0.7 us -> 4.91 us
    all_to_all x1, waiting for transfers between devices: 8.4 us -> 4.29 us  [body(): lax.all_to_all(con_sorted, 'blk', split_axis=1, concat_axis=0, tiled=True)]
    all_to_all x1, blocking collectives: 10.8 us -> 9.78 us  [body(): lax.all_to_all(terms, ('blk', 'ga'), split_axis=0, concat_axis=0, tiled=T...]
  transfers between devices with their start and end apart: 5 -> 5, of which waited for: 3 -> 4; matrix products, arithmetic and copies ran while one was open for 8% -> 14% of each run, Pallas kernels for 0% -> 0%
where the time goes in v1:
time: 73.9 us; the launch traced here: 73.6 us
  blocking collectives  32.2 us (44%)
  waiting for transfers between devices  15.8 us (21%)
  local copies, waits for them, and re-layouts  10.5 us (14%)
  starting transfers between devices  8.84 us (12%)
  matrix products  4.44 us (6%)
  other arithmetic  1.62 us (2%)
    all_gather x1, blocking collectives, body(): every_amp = lax.all_gather(amplitude, 'blk', axis=0, tiled=True)  22.4 us
    all_to_all x1, blocking collectives, body(): lax.all_to_all(terms, ('blk', 'ga'), split_axis=0, concat_axis=0, tiled=T...  9.78 us
    ppermute x3, waiting for transfers between devices, swap(): return lax.ppermute(value, axis, [(i, i ^ step) for i in range(size)])  7.51 us
    unnamed x11, local copies, waits for them, and re-layouts  4.91 us
    all_to_all x1, waiting for transfers between devices, body(): lax.all_to_all(con_sorted, 'blk', split_axis=1, concat_axis=0, tiled=True)  4.29 us
    all_to_all x1, waiting for transfers between devices, body(): lax.all_to_all(jnp.stack(jnp.split(zeta, lax.axis_size('blk'), axis=1)),...  3.98 us
    all_to_all x1, starting transfers between devices, body(): lax.all_to_all(jnp.stack(jnp.split(zeta, lax.axis_size('blk'), axis=1)),...  3.69 us
    all_to_all x1, starting transfers between devices, body(): lax.all_to_all(con_sorted, 'blk', split_axis=1, concat_axis=0, tiled=True)  3.49 us
  transfers between devices with their start and end apart: 5, of which 4 were waited for; matrix products, arithmetic and copies ran while one was open for 14% of the time, Pallas kernels for 0%

profile of v1, /device:TPU:0, one launch (start us, length us, event | category | flops | bytes accessed | tf_op | source)
XLA Modules:
  0.0 73.6 jit_solution(2614057251054318481)
XLA Ops:
  0.0 0.8 %select_reduce_fusion = s32[2,16]{1,0:T(2,128)S(1)} fusion(s32[2,16]{1,0:T(2,128)} %param.11), kind=kLoop, calls=%fused_computation.40 | loop fusion | flops 1504 | bytes 256 | tf_op jit(solution)/shard_map/reduce_sum | solution.py:14
  1.1 0.6 gather_fusion.2
  1.7 1.7 %gather_fusion.1 = bf16[32,16,512]{2,1,0:T(8,128)(2,1)S(1)} fusion(bf16[2,16,16,512]{3,2,1,0:T(8,128)(2,1)} %param.8, s32[32]{0:T(128)S(1)} %reshape.94), kind=kCustom, calls=%fused_computation.clone | custom fusion | bytes 1048832 | tf_op jit(solution)/shard_map/jit(take_along_axis)/gather | solution.py:29
  3.4 22.4 %all-gather = bf16[8,2,16]{2,1,0:T(2,128)(2,1)S(1)} all-gather(bf16[1,2,16]{2,1,0:T(2,128)(2,1)} %bitcast.135), channel_id=1, replica_groups=mesh['blk'=8,'ga'=4] {'blk'}, dimensions={0}, use_global_device_ids=true | all-gather | bytes 576 | tf_op jit(solution)/shard_map/all_gather | solution.py:27
  26.0 0.8 %copy.119 = bf16[2,16,16,512]{3,2,0,1:T(8,128)(2,1)} copy(bf16[2,16,16,512]{3,2,1,0:T(8,128)(2,1)S(1)} %get-tuple-element.9) | data formatting | bytes 1048576 | tf_op jit(solution)/shard_map/optimization_barrier | solution.py:30
  26.8 3.5 %all-to-all-start.1 = ((bf16[2,16,16,512]{3,2,0,1:T(8,128)(2,1)}), bf16[2,16,16,512]{3,2,0,1:T(8,128)(2,1)S(1)}, u32[]{:S(2)}, u32[]{:S(2)}) async-start(bf16[2,16,16,512]{3,2,0,1:T(8,128)(2,1)} %copy.119), calls=%async_computation.1 | async-start | bytes 1048576 | tf_op jit(solution)/shard_map/all_to_all | solution.py:31
  30.4 0.6 gather_fusion
  32.1 0.7 fusion.21
  32.8 0.7 fusion.20
  33.5 0.7 fusion.19
  34.2 0.7 fusion.18
  34.9 0.7 fusion.17
  35.5 0.7 fusion.16
  36.2 0.7 fusion.15
  36.9 4.3 %all-to-all-done.1 = bf16[2,16,16,512]{3,2,0,1:T(8,128)(2,1)S(1)} async-done(((bf16[2,16,16,512]{3,2,0,1:T(8,128)(2,1)}), bf16[2,16,16,512]{3,2,0,1:T(8,128)(2,1)S(1)}, u32[]{:S(2)}, u32[]{:S(2)}) %all-to-all-start.1) | async-done | bytes 524320 | tf_op jit(solution)/shard_map/all_to_all | solution.py:31
  41.3 1.6 %collective-permute-start.1 = (bf16[16,2,16,512]{3,2,0,1:T(8,128)(2,1)S(1)}, bf16[16,2,16,512]{3,2,0,1:T(8,128)(2,1)S(1)}, u32[]{:S(2)}, u32[]{:S(2)}) collective-permute-start(bf16[16,2,16,512]{3,2,0,1:T(8,128)(2,1)S(1)} %bitcast.131), channel_id=1, source_target_pairs={{0,2},{1,3},{2,0},{3,1},{4,6},{5,7},{6,4},{7,5},{8,10},{9,11},{10,... | collective-permute-start | bytes 1572872 | tf_op jit(solution)/shard_map/ppermute | solution.py:18
  42.9 0.7 fusion.14
  43.6 3.7 %all-to-all-start = ((bf16[8,2,2,16,512]{4,2,3,1,0:T(2,128)(2,1)}), bf16[8,2,2,16,512]{4,2,3,1,0:T(2,128)(2,1)S(1)}, u32[]{:S(2)}, u32[]{:S(2)}) async-start(bf16[8,2,2,16,512]{4,2,3,1,0:T(2,128)(2,1)} %fusion.14), calls=%async_computation | async-start | bytes 1048576 | tf_op jit(solution)/shard_map/all_to_all | solution.py:42
  47.3 1.8 %fusion.6 = f32[2,512,16,16]{1,3,2,0:T(8,128)S(1)} fusion(bf16[16,2,16,512]{3,2,0,1:T(8,128)(2,1)S(1)} %bitcast.132, bf16[2,4,512,512]{3,2,1,0:T(8,128)(2,1)} %bitcast.136, s32[]{:T(128)S(6)} %select_n.30), kind=kOutput, calls=%fused_computation.14 | convolution fusion | flops 268435456 | bytes 2621444 | tf_op jit(solution)/shard_map/kqxg,qgh->kqxh/dot_general | solution.py:50
  49.1 6.5 %collective-permute-done.1 = bf16[16,2,16,512]{3,2,0,1:T(8,128)(2,1)S(1)} collective-permute-done((bf16[16,2,16,512]{3,2,0,1:T(8,128)(2,1)S(1)}, bf16[16,2,16,512]{3,2,0,1:T(8,128)(2,1)S(1)}, u32[]{:S(2)}, u32[]{:S(2)}) %collective-permute-start.1) | collective-permute-done | bytes 524320 | tf_op jit(solution)/shard_map/ppermute | solution.py:18
  56.6 1.0 %collective-permute-done.2 = bf16[16,2,16,512]{3,2,0,1:T(8,128)(2,1)S(1)} collective-permute-done((bf16[16,2,16,512]{3,2,0,1:T(8,128)(2,1)S(1)}, bf16[16,2,16,512]{3,2,0,1:T(8,128)(2,1)S(1)}, u32[]{:S(2)}, u32[]{:S(2)}) %collective-permute-start.2) | collective-permute-done | bytes 524320 | tf_op jit(solution)/shard_map/ppermute | solution.py:18
  58.2 4.0 %all-to-all-done = bf16[8,2,2,16,512]{4,2,3,1,0:T(2,128)(2,1)S(1)} async-done(((bf16[8,2,2,16,512]{4,2,3,1,0:T(2,128)(2,1)}), bf16[8,2,2,16,512]{4,2,3,1,0:T(2,128)(2,1)S(1)}, u32[]{:S(2)}, u32[]{:S(2)}) %all-to-all-start) | async-done | bytes 524320 | tf_op jit(solution)/shard_map/all_to_all | solution.py:42
  62.1 0.9 %convolution_bitcast_fusion = f32[16,4,4]{2,1,0:T(4,128)S(1)} fusion(bf16[16,2,4,4,512]{4,3,2,0,1:T(4,128)(2,1)S(1)} %reshape.56, bf16[16,2,4,4,512]{4,1,3,2,0:T(2,128)(2,1)S(1)} %bitcast.129), kind=kOutput, calls=%fused_computation.10 | convolution fusion | flops 2097152 | bytes 1049600 | tf_op jit(solution)/shard_map/kqcyg,kqayg->kac/dot_general | solution.py:55
  63.2 9.8 %all_to_all.28 = f32[32,2,16]{2,1,0:T(2,128)S(1)} all-to-all(f32[32,2,16]{2,1,0:T(2,128)S(1)} %copy.128), channel_id=1, replica_groups=mesh['blk'=8,'ga'=4] {'blk','ga'}, dimensions={0} | all-to-all | bytes 8192 | tf_op jit(solution)/shard_map/all_to_all | solution.py:60
  (30 shorter events, 4.0 us)
Async XLA Ops:
  0.0 1.1 %copy-start = (bf16[2,16,16,512]{3,2,1,0:T(8,128)(2,1)S(1)}, bf16[2,16,16,512]{3,2,1,0:T(8,128)(2,1)}, u32[]{:S(2)}) copy-start(bf16[2,16,16,512]{3,2,1,0:T(8,128)(2,1)} %param.7) | copy-start | bytes 1572868
  26.8 14.4 %all-to-all-start.1 = ((bf16[2,16,16,512]{3,2,0,1:T(8,128)(2,1)}), bf16[2,16,16,512]{3,2,0,1:T(8,128)(2,1)S(1)}, u32[]{:S(2)}, u32[]{:S(2)}) async-start(bf16[2,16,16,512]{3,2,0,1:T(8,128)(2,1)} %copy.119), calls=%async_computation.1 | async-start | bytes 1048576 | tf_op jit(solution)/shard_map/all_to_all | solution.py:31
  41.3 14.4 %collective-permute-start = (bf16[16,2,16,512]{3,2,0,1:T(8,128)(2,1)S(1)}, bf16[16,2,16,512]{3,2,0,1:T(8,128)(2,1)S(1)}, u32[]{:S(2)}, u32[]{:S(2)}) collective-permute-start(bf16[16,2,16,512]{3,2,0,1:T(8,128)(2,1)S(1)} %bitcast.130), channel_id=1, source_target_pairs={{0,1},{1,0},{2,3},{3,2},{4,5},{5,4},{6,7},{7,6},{8,9},{9,8},{10,11... | collective-permute-start | bytes 1572872 | tf_op jit(solution)/shard_map/ppermute | solution.py:18
  41.3 14.3 %collective-permute-start.1 = (bf16[16,2,16,512]{3,2,0,1:T(8,128)(2,1)S(1)}, bf16[16,2,16,512]{3,2,0,1:T(8,128)(2,1)S(1)}, u32[]{:S(2)}, u32[]{:S(2)}) collective-permute-start(bf16[16,2,16,512]{3,2,0,1:T(8,128)(2,1)S(1)} %bitcast.131), channel_id=1, source_target_pairs={{0,2},{1,3},{2,0},{3,1},{4,6},{5,7},{6,4},{7,5},{8,10},{9,11},{10,... | collective-permute-start | bytes 1572872 | tf_op jit(solution)/shard_map/ppermute | solution.py:18
  43.6 18.5 %all-to-all-start = ((bf16[8,2,2,16,512]{4,2,3,1,0:T(2,128)(2,1)}), bf16[8,2,2,16,512]{4,2,3,1,0:T(2,128)(2,1)S(1)}, u32[]{:S(2)}, u32[]{:S(2)}) async-start(bf16[8,2,2,16,512]{4,2,3,1,0:T(2,128)(2,1)} %fusion.14), calls=%async_computation | async-start | bytes 1048576 | tf_op jit(solution)/shard_map/all_to_all | solution.py:42
  47.3 8.4 %copy-start.1 = (bf16[2,2048,512]{2,1,0:T(8,128)(2,1)S(1)}, bf16[2,2048,512]{2,1,0:T(8,128)(2,1)}, u32[]{:S(2)}) copy-start(bf16[2,2048,512]{2,1,0:T(8,128)(2,1)} %param.9) | copy-start | bytes 12582916
  55.7 1.9 %collective-permute-start.2 = (bf16[16,2,16,512]{3,2,0,1:T(8,128)(2,1)S(1)}, bf16[16,2,16,512]{3,2,0,1:T(8,128)(2,1)S(1)}, u32[]{:S(2)}, u32[]{:S(2)}) collective-permute-start(bf16[16,2,16,512]{3,2,0,1:T(8,128)(2,1)S(1)} %collective-permute-done.1), channel_id=1, source_target_pairs={{0,1},{1,0},{2,3},{3,2},{4,5},{5,4},{6,7},{7,6},{8,9},{9,8},{10,11... | collective-permute-start | bytes 1572872 | tf_op jit(solution)/shard_map/ppermute | solution.py:18
